TPU v7x, 32 devices: a whole 2x2x4 slice. The times are simulated.
32 devices in a mesh: batch: 8 (over z, y), space: 4 (over x, core).
Axes of the slice: x: 2, y: 2, z: 4, core: 2. Of those that a mesh axis runs over, the one named last changes fastest.
Arguments:
- features: bfloat16 [8, 48, 72, 1024], P('batch', 'space'), may hold values from -600 to 600
- depth_one: bfloat16 [3, 3, 1024], replicated, may hold values from -2 to 2
- gain_one: float32 [1024], replicated, may hold values from 0.25 to 1.75
- shift_one: float32 [1024], replicated, may hold values from -3 to 3
- point_one: bfloat16 [1024, 1536], replicated, may hold values from -0.1875 to 0.1875
- gain_two: float32 [1536], replicated, may hold values from 0.25 to 1.75
- shift_two: float32 [1536], replicated, may hold values from -3 to 3
- depth_two: bfloat16 [3, 3, 1536], replicated, may hold values from -2 to 2
- gain_three: float32 [1536], replicated, may hold values from 0.25 to 1.75
- shift_three: float32 [1536], replicated, may hold values from -3 to 3
- point_two: bfloat16 [1536, 2048], replicated, may hold values from -0.15625 to 0.15625
- gain_four: float32 [2048], replicated, may hold values from 0.25 to 1.75
- shift_four: float32 [2048], replicated, may hold values from -3 to 3
Outputs:
- exit_map: bfloat16 [8, 48, 72, 2048], P('batch', 'space')
All inputs are finite; a program needn't handle non-finite values.
Results may differ from a plain program's by a relative error of at most 0.0079.
Values may be sent and summed in bfloat16 or wider, within the bound.
A program may use at most 64 MiB of HBM per device.

v0:
```python
import functools

import jax
import jax.numpy as jnp
from jax import lax
from jax.experimental import pallas as pl
from jax.experimental.pallas import tpu as pltpu
from jax.sharding import PartitionSpec as P

RATE = 2
PIECES = 4
EPS = 1e-05
LANES = 128
PAD = 8
NCOL = 256
MESH = pl.DeviceIdType.MESH
F32 = jnp.float32
BF16 = jnp.bfloat16


def block_rows(pixels):
    for rows in (144, 96, 48, 32, 16):
        if pixels % rows == 0:
            return rows
    return pixels


def kernel(
    n_space,
    n_batch,
    x_hbm,
    w1_hbm,
    w2_hbm,
    d1_ref,
    d2_ref,
    g1_ref,
    b1_ref,
    g2_ref,
    b2_ref,
    g3_ref,
    b3_ref,
    g4_ref,
    b4_ref,
    fourth,
    mean_out,
    fac_out,
    shift_out,
    x_ref,
    w1_ref,
    w2_ref,
    halo1,
    edge2,
    halo2,
    xp,
    first,
    act1,
    second,
    act3,
    par_ref,
    sa0,
    sa1,
    sa2,
    sa3,
    sa4,
    sa5,
    sa6,
    sb0,
    sb1,
    sb2,
    sb3,
    sb4,
    sb5,
    sb6,
    coef,
    load_sem,
    h1_send,
    h1_recv,
    h2_send,
    h2_recv,
    a_send,
    a_recv,
    b_send,
    b_recv,
):
    rows, cols, c_in = x_hbm.shape
    c_mid = w1_hbm.shape[1]
    c_out = w2_hbm.shape[1]
    pixels = rows * cols
    edge = RATE * cols
    total = float(pixels * n_space * n_batch)
    step = block_rows(pixels)
    n_in, n_mid, n_out = c_in // LANES, c_mid // LANES, c_out // LANES
    sp = lax.axis_index("space")
    bt = lax.axis_index("batch")
    has_top = sp > 0
    has_bot = sp < n_space - 1
    sa = (sa0, sa1, sa2, sa3, sa4, sa5, sa6)
    sb = (sb0, sb1, sb2, sb3, sb4, sb5, sb6)

    load_x = pltpu.make_async_copy(x_hbm, x_ref, load_sem.at[0])
    load_w1 = pltpu.make_async_copy(w1_hbm, w1_ref, load_sem.at[1])
    load_w2 = pltpu.make_async_copy(w2_hbm, w2_ref, load_sem.at[2])

    barrier = pltpu.get_barrier_semaphore()
    for d in range(1, n_space):
        pl.semaphore_signal(
            barrier, inc=1, device_id={"space": lax.rem(sp + d, n_space)}, device_id_type=MESH
        )
    for d in range(1, n_batch):
        pl.semaphore_signal(
            barrier, inc=1, device_id={"batch": lax.rem(bt + d, n_batch)}, device_id_type=MESH
        )
    load_x.start()
    load_w1.start()
    load_w2.start()

    def clear(j, carry):
        for r in range(rows + 2 * RATE):
            xp[j, r, 0:PAD, :] = jnp.zeros((PAD, LANES), F32)
            xp[j, r, PAD + cols : PAD + cols + PAD, :] = jnp.zeros((PAD, LANES), F32)
        return carry

    lax.fori_loop(0, c_mid // LANES, clear, 0)
    at = 0
    for ref in (g1_ref, b1_ref, g2_ref, b2_ref, g3_ref, b3_ref, g4_ref, b4_ref):
        for j in range(ref.shape[0] // LANES):
            par_ref[at : at + 1, :] = ref[j * LANES : (j + 1) * LANES].reshape(1, LANES)
            at += 1
    load_x.wait()
    pl.semaphore_wait(barrier, n_space - 1 + n_batch - 1)

    wide_in = c_in // PIECES

    def up1(p):
        lanes = pl.ds(p * wide_in, wide_in)
        return pltpu.make_async_remote_copy(
            src_ref=x_ref.at[pl.ds(rows - RATE, RATE), :, lanes],
            dst_ref=halo1.at[0, :, :, lanes],
            send_sem=h1_send.at[0, p],
            recv_sem=h1_recv.at[0, p],
            device_id={"space": sp + 1},
            device_id_type=MESH,
        )

    def down1(p):
        lanes = pl.ds(p * wide_in, wide_in)
        return pltpu.make_async_remote_copy(
            src_ref=x_ref.at[pl.ds(0, RATE), :, lanes],
            dst_ref=halo1.at[1, :, :, lanes],
            send_sem=h1_send.at[1, p],
            recv_sem=h1_recv.at[1, p],
            device_id={"space": sp - 1},
            device_id_type=MESH,
        )

    for p in range(PIECES):

        @pl.when(has_bot)
        def _():
            up1(p).start()

        @pl.when(has_top)
        def _():
            down1(p).start()

    @pl.when(jnp.logical_not(has_top))
    def _():
        halo1[0] = jnp.zeros(halo1.shape[1:], BF16)

    @pl.when(jnp.logical_not(has_bot))
    def _():
        halo1[1] = jnp.zeros(halo1.shape[1:], BF16)

    def taps(d_ref, lanes):
        return [
            [d_ref[a, b : b + 1, lanes].astype(F32) for b in range(3)] for a in range(3)
        ]

    def conv_row(j, r, filt):
        acc = None
        for a in range(3):
            for b in range(3):
                term = xp[j, r + RATE * a, pl.ds(PAD + RATE * (b - 1), cols), :] * filt[a][b]
                acc = term if acc is None else acc + term
        return acc

    def lanes_of(j):
        return pl.ds(pl.multiple_of(j * LANES, LANES), LANES)

    def fold(v):
        s = v[0:8]
        for k in range(1, v.shape[0] // 8):
            s = s + v[8 * k : 8 * k + 8]
        return s

    def conv_rows(j, row_list, d_ref, dst, s1, s2):
        lanes = lanes_of(j)
        filt = taps(d_ref, lanes)
        for r in row_list:
            y = conv_row(j, r, filt)
            dst[r * cols : (r + 1) * cols, lanes] = y
            s1 = s1 + fold(y)
            s2 = s2 + fold(y * y)
        return s1, s2

    def put_stats(buf, slot, row, count, s1, s2):
        buf[slot, pl.ds(row, 1), :] = jnp.sum(s1, axis=0, keepdims=True)
        buf[slot, pl.ds(row + count, 1), :] = jnp.sum(s2, axis=0, keepdims=True)

    def exchange_a(i, d):
        return pltpu.make_async_remote_copy(
            src_ref=sa[i].at[sp],
            dst_ref=sa[i].at[sp],
            send_sem=a_send.at[i, d - 1],
            recv_sem=a_recv.at[i, d - 1],
            device_id={"space": lax.rem(sp + d, n_space)},
            device_id_type=MESH,
        )

    def exchange_b(i, d):
        return pltpu.make_async_remote_copy(
            src_ref=sb[i].at[bt],
            dst_ref=sb[i].at[bt],
            send_sem=b_send.at[i, d - 1],
            recv_sem=b_recv.at[i, d - 1],
            device_id={"batch": lax.rem(bt + d, n_batch)},
            device_id_type=MESH,
        )

    def start(i):
        for d in range(1, n_space):
            exchange_a(i, d).start()

    def relay(i):
        for d in range(1, n_space):
            exchange_a(i, d).wait_recv()
        s = sa[i][0]
        for k in range(1, n_space):
            s = s + sa[i][k]
        sb[i][bt] = s
        for d in range(1, n_batch):
            exchange_b(i, d).start()

    def finish(i, j0, count, at, full):
        for d in range(1, n_batch):
            exchange_b(i, d).wait_recv()
        s = sb[i][0]
        for k in range(1, n_batch):
            s = s + sb[i][k]
        mean = s[:count] / total
        var = s[count:] / total - mean * mean
        fac = par_ref[at + j0 : at + j0 + count] * lax.rsqrt(var + EPS)
        coef[0, j0 : j0 + count] = mean
        coef[1, j0 : j0 + count] = fac
        coef[2, j0 : j0 + count] = par_ref[at + full + j0 : at + full + j0 + count]
        for d in range(1, n_space):
            exchange_a(i, d).wait_send()
        for d in range(1, n_batch):
            exchange_b(i, d).wait_send()

    def normal(v, j):
        return jnp.maximum(
            (v - coef[0, pl.ds(j, 1), :]) * coef[1, pl.ds(j, 1), :] + coef[2, pl.ds(j, 1), :], 0.0
        ).astype(BF16)

    zero8 = jnp.zeros((8, LANES), F32)
    inner = list(range(RATE, rows - RATE))
    outer = list(range(RATE)) + list(range(rows - RATE, rows))


    def conv1_inner(j, carry):
        lanes = lanes_of(j)
        for r in range(rows):
            xp[j, r + RATE, PAD : PAD + cols, :] = x_ref[r, :, lanes].astype(F32)
        s1, s2 = conv_rows(j, inner, d1_ref, first, zero8, zero8)
        coef[3, pl.ds(pl.multiple_of(j * 8, 8), 8), :] = s1
        coef[4, pl.ds(pl.multiple_of(j * 8, 8), 8), :] = s2
        return carry

    lax.fori_loop(0, n_in, conv1_inner, 0)

    half_in = n_in // 2

    def conv1_outer(buf, j0):
        def body(j, carry):
            lanes = lanes_of(j)
            for r in range(RATE):
                xp[j, r, PAD : PAD + cols, :] = halo1[0, r, :, lanes].astype(F32)
                xp[j, rows + RATE + r, PAD : PAD + cols, :] = halo1[1, r, :, lanes].astype(F32)
            s1 = coef[3, pl.ds(pl.multiple_of(j * 8, 8), 8), :]
            s2 = coef[4, pl.ds(pl.multiple_of(j * 8, 8), 8), :]
            s1, s2 = conv_rows(j, outer, d1_ref, first, s1, s2)
            put_stats(buf, sp, j - j0, half_in, s1, s2)
            return carry

        return body

    for p in range(PIECES):

        @pl.when(has_top)
        def _():
            up1(p).wait_recv()

        @pl.when(has_bot)
        def _():
            down1(p).wait_recv()

        g = 2 * p // PIECES
        body = conv1_outer(sa[g], g * half_in)
        lax.fori_loop(p * n_in // PIECES, (p + 1) * n_in // PIECES, body, 0)
        if 2 * (p + 1) % PIECES == 0:
            start(g)

    relay(0)
    relay(1)
    finish(0, 0, half_in, 0, n_in)

    for p in range(PIECES):

        @pl.when(has_bot)
        def _():
            up1(p).wait_send()

        @pl.when(has_top)
        def _():
            down1(p).wait_send()

    def norm_to(src, dst, j0, j1):
        def body(j, carry):
            lanes = lanes_of(j)
            for k in range(pixels // step):
                span = slice(k * step, (k + 1) * step)
                dst[span, lanes] = normal(src[span, lanes], j)
            return carry

        lax.fori_loop(j0, j1, body, 0)

    def up2(n):
        return pltpu.make_async_remote_copy(
            src_ref=edge2.at[0, n],
            dst_ref=halo2.at[0, n],
            send_sem=h2_send.at[0, n],
            recv_sem=h2_recv.at[0, n],
            device_id={"space": sp + 1},
            device_id_type=MESH,
        )

    def down2(n):
        return pltpu.make_async_remote_copy(
            src_ref=edge2.at[1, n],
            dst_ref=halo2.at[1, n],
            send_sem=h2_send.at[1, n],
            recv_sem=h2_recv.at[1, n],
            device_id={"space": sp - 1},
            device_id_type=MESH,
        )

    per = NCOL // LANES

    def project_first(act, w_ref, dst, k1):
        def body(n, carry):
            wide = pl.ds(pl.multiple_of(n * NCOL, NCOL), NCOL)
            dst[:, wide] = jnp.dot(act[:, :k1], w_ref[:k1, wide], preferred_element_type=F32)
            return carry

        lax.fori_loop(0, dst.shape[1] // NCOL, body, 0)

    def project_rest(act, w_ref, dst, k0, n0, n1, buf, after):
        count = (n1 - n0) * per

        def body(n, carry):
            wide = pl.ds(pl.multiple_of(n * NCOL, NCOL), NCOL)
            y = jnp.dot(act[:, k0:], w_ref[k0:, wide], preferred_element_type=F32)
            y = y + dst[:, wide]
            dst[:, wide] = y
            s1 = fold(y)
            s2 = fold(y * y)
            for q in range(per):
                part = slice(q * LANES, (q + 1) * LANES)
                put_stats(buf, sp, (n - n0) * per + q, count, s1[:, part], s2[:, part])
            after(n, y)
            return carry

        lax.fori_loop(n0, n1, body, 0)

    n_wide = c_mid // NCOL
    early = n_wide // 2

    def send_edges(n, y):
        edge2[0, n] = y[pixels - edge :].astype(BF16)
        edge2[1, n] = y[:edge].astype(BF16)

        @pl.when(jnp.logical_and(has_bot, n < early))
        def _():
            up2(n).start()

        @pl.when(jnp.logical_and(has_top, n < early))
        def _():
            down2(n).start()

    def send_late():
        def body(n, carry):
            @pl.when(has_bot)
            def _():
                up2(n).start()

            @pl.when(has_top)
            def _():
                down2(n).start()

            return carry

        lax.fori_loop(early, n_wide, body, 0)

    half_mid = n_mid // 2
    norm_to(first, act1, 0, half_in)
    load_w1.wait()
    project_first(act1, w1_ref, second, half_in * LANES)
    finish(1, half_in, half_in, 0, n_in)
    norm_to(first, act1, half_in, n_in)
    project_rest(act1, w1_ref, second, half_in * LANES, 0, early, sa2, send_edges)
    start(2)
    project_rest(act1, w1_ref, second, half_in * LANES, early, n_wide, sa3, send_edges)
    start(3)
    send_late()
    relay(2)
    relay(3)

    def wait_edges(n, carry):
        @pl.when(has_top)
        def _():
            up2(n).wait_recv()

        @pl.when(has_bot)
        def _():
            down2(n).wait_recv()

        return carry

    @pl.when(jnp.logical_not(has_top))
    def _():
        halo2[0] = jnp.zeros(halo2.shape[1:], BF16)

    @pl.when(jnp.logical_not(has_bot))
    def _():
        halo2[1] = jnp.zeros(halo2.shape[1:], BF16)


    def conv2(buf, n0, n, carry):
        for q in range(NCOL // LANES):
            j = n * (NCOL // LANES) + q
            lanes = lanes_of(j)
            part = slice(q * LANES, (q + 1) * LANES)
            for r in range(rows):
                v = normal(second[r * cols : (r + 1) * cols, lanes], j)
                xp[j, r + RATE, PAD : PAD + cols, :] = v.astype(F32)
            top = normal(halo2[0, n, :, part].astype(F32), j).astype(F32)
            top = jnp.where(has_top, top, 0.0)
            bot = normal(halo2[1, n, :, part].astype(F32), j).astype(F32)
            bot = jnp.where(has_bot, bot, 0.0)
            for r in range(RATE):
                xp[j, r, PAD : PAD + cols, :] = top[r * cols : (r + 1) * cols]
                xp[j, rows + RATE + r, PAD : PAD + cols, :] = bot[r * cols : (r + 1) * cols]
            s1, s2 = conv_rows(j, list(range(rows)), d2_ref, second, zero8, zero8)
            put_stats(buf, sp, j - n0 * per, half_mid, s1, s2)
        return carry

    at2, at3 = 2 * n_in, 2 * n_in + 2 * n_mid
    finish(2, 0, half_mid, at2, n_mid)
    lax.fori_loop(0, early, wait_edges, 0)
    lax.fori_loop(0, early, functools.partial(conv2, sa4, 0), 0)
    start(4)
    finish(3, half_mid, half_mid, at2, n_mid)
    lax.fori_loop(early, n_wide, wait_edges, 0)
    lax.fori_loop(early, n_wide - 1, functools.partial(conv2, sa5, early), 0)
    relay(4)
    lax.fori_loop(n_wide - 1, n_wide, functools.partial(conv2, sa5, early), 0)
    start(5)
    finish(4, 0, half_mid, at3, n_mid)
    relay(5)

    norm_to(second, act3, 0, half_mid)
    load_w2.wait()
    project_first(act3, w2_ref, fourth, half_mid * LANES)
    finish(5, half_mid, half_mid, at3, n_mid)
    norm_to(second, act3, half_mid, n_mid)
    project_rest(act3, w2_ref, fourth, half_mid * LANES, 0, c_out // NCOL, sa6, lambda n, y: None)
    start(6)
    relay(6)
    finish(6, 0, n_out, 2 * n_in + 4 * n_mid, n_out)

    for q, ref in enumerate((mean_out, fac_out, shift_out)):
        for j in range(n_out):
            ref[0:1, j * LANES : (j + 1) * LANES] = coef[q, j : j + 1, :]

    def drain(n, carry):
        @pl.when(has_bot)
        def _():
            up2(n).wait_send()

        @pl.when(has_top)
        def _():
            down2(n).wait_send()

        return carry

    lax.fori_loop(0, n_wide, drain, 0)


def per_device(
    features,
    depth_one,
    gain_one,
    shift_one,
    point_one,
    gain_two,
    shift_two,
    depth_two,
    gain_three,
    shift_three,
    point_two,
    gain_four,
    shift_four,
):
    samples, span_rows, cols, c_in = features.shape
    rows = samples * span_rows
    assert samples == 1
    c_mid = point_one.shape[1]
    c_out = point_two.shape[1]
    pixels = rows * cols
    n_space = lax.axis_size("space")
    n_batch = lax.axis_size("batch")
    n_in, n_mid, n_out = c_in // LANES, c_mid // LANES, c_out // LANES
    any_spec = pl.BlockSpec(memory_space=pl.ANY)
    vmem = pl.BlockSpec(memory_space=pltpu.VMEM)
    counts = (n_in // 2,) * 2 + (n_mid // 2,) * 4 + (n_out,)
    edge = RATE * cols
    n_wide = c_mid // NCOL
    coef_rows = max(n_out, 8 * n_in)
    DMA = pltpu.SemaphoreType.DMA
    fourth, mean, fac, shift = pl.pallas_call(
        functools.partial(kernel, n_space, n_batch),
        out_shape=(
            pltpu.VMEM((pixels, c_out), F32),
            jax.ShapeDtypeStruct((1, c_out), F32),
            jax.ShapeDtypeStruct((1, c_out), F32),
            jax.ShapeDtypeStruct((1, c_out), F32),
        ),
        in_specs=[any_spec] * 3 + [vmem] * 10,
        out_specs=(vmem,) * 4,
        scratch_shapes=[
            pltpu.VMEM((rows, cols, c_in), BF16),
            pltpu.VMEM((c_in, c_mid), BF16),
            pltpu.VMEM((c_mid, c_out), BF16),
            pltpu.VMEM((2, RATE, cols, c_in), BF16),
            pltpu.VMEM((2, n_wide, edge, NCOL), BF16),
            pltpu.VMEM((2, n_wide, edge, NCOL), BF16),
            pltpu.VMEM((n_mid, rows + 2 * RATE, cols + 2 * PAD, LANES), F32),
            pltpu.VMEM((pixels, c_in), F32),
            pltpu.VMEM((pixels, c_in), BF16),
            pltpu.VMEM((pixels, c_mid), F32),
            pltpu.VMEM((pixels, c_mid), BF16),
            pltpu.VMEM((2 * sum((n_in, n_mid, n_mid, n_out)), LANES), F32),
        ]
        + [pltpu.VMEM((n_space, 2 * c, LANES), F32) for c in counts]
        + [pltpu.VMEM((n_batch, 2 * c, LANES), F32) for c in counts]
        + [
            pltpu.VMEM((5, coef_rows, LANES), F32),
            DMA((3,)),
            DMA((2, PIECES)),
            DMA((2, PIECES)),
            DMA((2, n_wide)),
            DMA((2, n_wide)),
            DMA((7, n_space - 1)),
            DMA((7, n_space - 1)),
            DMA((7, n_batch - 1)),
            DMA((7, n_batch - 1)),
        ],
        compiler_params=pltpu.CompilerParams(
            collective_id=0, has_side_effects=True, vmem_limit_bytes=56 * 1024 * 1024
        ),
        name="exit_block",
    )(
        features.reshape(rows, cols, c_in),
        point_one,
        point_two,
        depth_one,
        depth_two,
        *(
            v
            for v in (
                gain_one,
                shift_one,
                gain_two,
                shift_two,
                gain_three,
                shift_three,
                gain_four,
                shift_four,
            )
        ),
    )
    out = jnp.maximum((fourth - mean) * fac + shift, 0.0).astype(BF16)
    return out.reshape(samples, span_rows, cols, c_out)


def solution(mesh):
    return jax.shard_map(
        per_device,
        mesh=mesh,
        in_specs=(P("batch", "space", None, None),) + (P(),) * 12,
        out_specs=P("batch", "space", None, None),
        check_vma=False,
    )
```

profile of v0, /device:TPU:0, one launch (start us, length us, event | category | flops | bytes accessed | tf_op | source)
XLA Modules:
  0.0 63.0 jit_solution(8779906596796335690)
XLA Ops:
  0.0 59.3 %exit_block.1 = (f32[864,2048]{1,0:T(8,128)S(1)}, f32[1,2048]{1,0:T(1,128)}, f32[1,2048]{1,0:T(1,128)}, f32[1,2048]{1,0:T(1,128)}) custom-call(bf16[12,72,1024]{2,1,0:T(8,128)(2,1)} %bitcast.5, bf16[1024,1536]{1,0:T(8,128)(2,1)} %w1_hbm.1, bf16[1536,2048]{1,0:T(8,128)(2,1)} %w2_hbm.1, bf16[3,3,1024]{2,1,0:T(4,128)(2,1)} %d1_ref.1, ...), custom_call_target="tpu_custom_call" | custom-call | tf_op jit(solution)/shard_map/exit_block/pallas_call | solution.py:541
  59.3 3.7 %maximum_convert_fusion = bf16[864,2048]{1,0:T(8,128)(2,1)} fusion(f32[864,2048]{1,0:T(8,128)S(1)} %get-tuple-element.9, f32[2048]{0:T(1024)} %bitcast.8, f32[2048]{0:T(1024)} %bitcast.7, f32[2048]{0:T(1024)} %bitcast.6), kind=kLoop, calls=%fused_computation | loop fusion | flops 8847360 | bytes 10641408 | tf_op jit(solution)/shard_map/convert_element_type | solution.py:603
where the time goes:
time: 63.2 us; the launch traced here: 63 us
  Pallas kernels  59.3 us (94%)
  other arithmetic  3.68 us (6%)
    pallas_call x1, Pallas kernels, per_device(): pl.pallas_call(functools.partial(kernel, n_space, n_batch), out_shape=(pl...  59.3 us
    convert_element_type x1, other arithmetic, per_device(): out = jnp.maximum((fourth - mean) * fac + shift, 0.0).astype(BF16)  3.68 us

commit v1 on v0

v1 whole, which is shorter than its diff:
```python
import functools

import jax
import jax.numpy as jnp
from jax import lax
from jax.experimental import pallas as pl
from jax.experimental.pallas import tpu as pltpu
from jax.sharding import PartitionSpec as P

RATE = 2
EPS = 1e-05
LANES = 128
PAD = 8
CHUNK = 256
PER = CHUNK // LANES
LAG = 4
MESH = pl.DeviceIdType.MESH
F32 = jnp.float32
BF16 = jnp.bfloat16
scope = jax.named_scope


def block_rows(pixels):
    for rows in (144, 96, 48, 32, 16):
        if pixels % rows == 0:
            return rows
    return pixels


def kernel(
    n_space,
    n_batch,
    x_hbm,
    w1_hbm,
    w2_hbm,
    d1_ref,
    d2_ref,
    g1_ref,
    b1_ref,
    g2_ref,
    b2_ref,
    g3_ref,
    b3_ref,
    g4_ref,
    b4_ref,
    out,
    x_ref,
    w1_ref,
    w2_ref,
    halo1,
    edge2,
    halo2,
    xp,
    first,
    act1,
    second,
    act3,
    fourth,
    par,
    coef,
    acc,
    pa,
    pb,
    x_sem,
    w_sem,
    h1_send,
    h1_recv,
    h2_send,
    h2_recv,
    a_send,
    a_recv,
    b_send,
    b_recv,
):
    rows, cols, c_in = x_hbm.shape
    c_mid = w1_hbm.shape[1]
    c_out = w2_hbm.shape[1]
    pixels = rows * cols
    edge = RATE * cols
    total = float(pixels * n_space * n_batch)
    step = block_rows(pixels)
    k_in, k_mid, k_out = c_in // CHUNK, c_mid // CHUNK, c_out // CHUNK
    at1, at2, at3, at4 = 0, k_in, k_in + k_mid, k_in + 2 * k_mid
    n_sum = at4 + k_out
    half = n_space // 2
    n_far = n_batch * half
    sp = lax.axis_index("space")
    bt = lax.axis_index("batch")
    side = lax.rem(sp, 2)
    mine = bt * half + sp // 2
    partner = sp + 1 - 2 * side
    has_top = sp > 0
    has_bot = sp < n_space - 1
    odd = side == 1
    cross = jnp.where(odd, sp + 1, sp - 1)
    has_cross = jnp.logical_or(
        jnp.logical_and(odd, has_bot), jnp.logical_and(jnp.logical_not(odd), has_top)
    )

    def far(d):
        at = lax.rem(mine + d, n_far)
        return {"batch": at // half, "space": lax.rem(at, half) * 2 + side}

    def each_far(body):
        if n_far <= 16:
            for d in range(1, n_far):
                body(d)
        else:

            def step_far(d, carry):
                body(d)
                return carry

            lax.fori_loop(1, n_far, step_far, 0)

    spans = [(0, RATE), (rows - RATE, RATE)]
    load_edges = [
        pltpu.make_async_copy(
            x_hbm.at[pl.ds(s, n)], x_ref.at[pl.ds(s, n)], x_sem.at[q]
        )
        for q, (s, n) in enumerate(spans)
    ]

    def load_inner(c):
        block = (pl.ds(RATE, rows - 2 * RATE), slice(None), pl.ds(c * CHUNK, CHUNK))
        return pltpu.make_async_copy(x_hbm.at[block], x_ref.at[block], x_sem.at[2 + c])

    load_w1 = pltpu.make_async_copy(w1_hbm, w1_ref, w_sem.at[0])
    load_w2 = pltpu.make_async_copy(w2_hbm, w2_ref, w_sem.at[1])

    for cp in load_edges:
        cp.start()
    for c in range(k_in):
        load_inner(c).start()

    barrier = pltpu.get_barrier_semaphore()
    pl.semaphore_signal(barrier, inc=1, device_id={"space": partner}, device_id_type=MESH)

    @pl.when(has_cross)
    def _():
        pl.semaphore_signal(barrier, inc=1, device_id={"space": cross}, device_id_type=MESH)

    each_far(
        lambda d: pl.semaphore_signal(barrier, inc=1, device_id=far(d), device_id_type=MESH)
    )

    def clear(j, carry):
        for r in range(rows + 2 * RATE):
            xp[j, r, 0:PAD, :] = jnp.zeros((PAD, LANES), F32)
            xp[j, r, PAD + cols : PAD + cols + PAD, :] = jnp.zeros((PAD, LANES), F32)
        return carry

    with scope("P00clear"):
        lax.fori_loop(0, c_mid // LANES, clear, 0)
        at = 0
        for g_ref, b_ref in ((g1_ref, b1_ref), (g2_ref, b2_ref), (g3_ref, b3_ref), (g4_ref, b4_ref)):
            for c in range(g_ref.shape[0] // CHUNK):
                for q in range(PER):
                    lanes = slice(c * CHUNK + q * LANES, c * CHUNK + (q + 1) * LANES)
                    par[at, q : q + 1, :] = g_ref[lanes].reshape(1, LANES)
                    par[at, PER + q : PER + q + 1, :] = b_ref[lanes].reshape(1, LANES)
                at += 1
    with scope("P01edgewait"):
        for cp in load_edges:
            cp.wait()
    with scope("P02barrier"):
        pl.semaphore_wait(barrier, n_far + jnp.where(has_cross, 1, 0))

    def up1(p):
        lanes = pl.ds(p * CHUNK, CHUNK)
        return pltpu.make_async_remote_copy(
            src_ref=x_ref.at[pl.ds(rows - RATE, RATE), :, lanes],
            dst_ref=halo1.at[0, :, :, lanes],
            send_sem=h1_send.at[0, p],
            recv_sem=h1_recv.at[0, p],
            device_id={"space": sp + 1},
            device_id_type=MESH,
        )

    def down1(p):
        lanes = pl.ds(p * CHUNK, CHUNK)
        return pltpu.make_async_remote_copy(
            src_ref=x_ref.at[pl.ds(0, RATE), :, lanes],
            dst_ref=halo1.at[1, :, :, lanes],
            send_sem=h1_send.at[1, p],
            recv_sem=h1_recv.at[1, p],
            device_id={"space": sp - 1},
            device_id_type=MESH,
        )

    def up2(n):
        return pltpu.make_async_remote_copy(
            src_ref=edge2.at[0, n],
            dst_ref=halo2.at[0, n],
            send_sem=h2_send.at[0, n],
            recv_sem=h2_recv.at[0, n],
            device_id={"space": sp + 1},
            device_id_type=MESH,
        )

    def down2(n):
        return pltpu.make_async_remote_copy(
            src_ref=edge2.at[1, n],
            dst_ref=halo2.at[1, n],
            send_sem=h2_send.at[1, n],
            recv_sem=h2_recv.at[1, n],
            device_id={"space": sp - 1},
            device_id_type=MESH,
        )

    def send_rows(up, down, p):
        @pl.when(has_bot)
        def _():
            up(p).start()

        @pl.when(has_top)
        def _():
            down(p).start()

    def recv_rows(up, down, p):
        @pl.when(has_top)
        def _():
            up(p).wait_recv()

        @pl.when(has_bot)
        def _():
            down(p).wait_recv()

    def sent_rows(up, down, p):
        @pl.when(has_bot)
        def _():
            up(p).wait_send()

        @pl.when(has_top)
        def _():
            down(p).wait_send()

    for p in range(k_in):
        send_rows(up1, down1, p)

    for halo in (halo1, halo2):

        @pl.when(jnp.logical_not(has_top))
        def _():
            halo[0] = jnp.zeros(halo.shape[1:], BF16)

        @pl.when(jnp.logical_not(has_bot))
        def _():
            halo[1] = jnp.zeros(halo.shape[1:], BF16)

    def near_sum(i):
        return pltpu.make_async_remote_copy(
            src_ref=pa.at[i, 0],
            dst_ref=pa.at[i, 1],
            send_sem=a_send.at[i],
            recv_sem=a_recv.at[i],
            device_id={"space": partner},
            device_id_type=MESH,
        )

    def far_sum(i, d):
        return pltpu.make_async_remote_copy(
            src_ref=pb.at[i, mine],
            dst_ref=pb.at[i, mine],
            send_sem=b_send.at[i],
            recv_sem=b_recv.at[i],
            device_id=far(d),
            device_id_type=MESH,
        )

    def far_all(i):
        block = pb.at[i, pl.ds(0, n_far - 1)]
        return pltpu.make_async_remote_copy(
            src_ref=block,
            dst_ref=block,
            send_sem=b_send.at[i],
            recv_sem=b_recv.at[i],
            device_id=far(1),
            device_id_type=MESH,
        )

    def start(i):
        near_sum(i).start()

    def relay(i):
        near_sum(i).wait_recv()
        pb[i, mine] = pa[i, 0] + pa[i, 1]
        each_far(lambda d: far_sum(i, d).start())

    def finish(i):
        far_all(i).wait_recv()
        parts = [pb[i, k] for k in range(n_far)]
        while len(parts) > 1:
            parts = [a + b for a, b in zip(parts[0::2], parts[1::2])] + (
                parts[-1:] if len(parts) % 2 else []
            )
        s = parts[0] * (1.0 / total)
        mean = s[:PER]
        var = s[PER:] - mean * mean
        p = par[i]
        coef[i, 0:PER] = mean
        coef[i, PER : 2 * PER] = p[:PER] * lax.rsqrt(var + EPS)

    def normal(v, i, q):
        mean = coef[i, pl.ds(q, 1), :]
        fac = coef[i, pl.ds(PER + q, 1), :]
        return jnp.maximum((v - mean) * fac + par[i, pl.ds(PER + q, 1), :], 0.0).astype(BF16)

    def taps(d_ref, lanes):
        return [
            [d_ref[a, b : b + 1, lanes].astype(F32) for b in range(3)] for a in range(3)
        ]

    def conv_row(j, r, filt):
        y = None
        for a in range(3):
            for b in range(3):
                term = xp[j, r + RATE * a, pl.ds(PAD + RATE * (b - 1), cols), :] * filt[a][b]
                y = term if y is None else y + term
        return y

    def lanes_of(j):
        return pl.ds(pl.multiple_of(j * LANES, LANES), LANES)

    def wide_of(n):
        return pl.ds(pl.multiple_of(n * CHUNK, CHUNK), CHUNK)

    def fold(v):
        s = v[0:8]
        for k in range(1, v.shape[0] // 8):
            s = s + v[8 * k : 8 * k + 8]
        return s

    def conv_rows(j, row_list, d_ref, dst, s1, s2):
        lanes = lanes_of(j)
        filt = taps(d_ref, lanes)
        for r in row_list:
            y = conv_row(j, r, filt)
            dst[r * cols : (r + 1) * cols, lanes] = y
            s1 = s1 + fold(y)
            s2 = s2 + fold(y * y)
        return s1, s2

    def put_stats(i, q, s1, s2):
        pa[i, 0, pl.ds(q, 1), :] = jnp.sum(s1, axis=0, keepdims=True)
        pa[i, 0, pl.ds(PER + q, 1), :] = jnp.sum(s2, axis=0, keepdims=True)

    zero8 = jnp.zeros((8, LANES), F32)
    inner = list(range(RATE, rows - RATE))
    outer = list(range(RATE)) + list(range(rows - RATE, rows))

    def conv1_inner(j, carry):
        lanes = lanes_of(j)
        for r in range(rows):
            xp[j, r + RATE, PAD : PAD + cols, :] = x_ref[r, :, lanes].astype(F32)
        s1, s2 = conv_rows(j, inner, d1_ref, first, zero8, zero8)
        acc[0, j] = s1
        acc[1, j] = s2
        return carry

    for c in range(k_in):
        with scope("P03conv1inner"):
            load_inner(c).wait()
            lax.fori_loop(c * PER, (c + 1) * PER, conv1_inner, 0)
    load_w1.start()
    load_w2.start()

    def conv1_outer(i):
        def body(q, carry):
            j = i * PER + q
            lanes = lanes_of(j)
            for r in range(RATE):
                xp[j, r, PAD : PAD + cols, :] = halo1[0, r, :, lanes].astype(F32)
                xp[j, rows + RATE + r, PAD : PAD + cols, :] = halo1[1, r, :, lanes].astype(F32)
            s1, s2 = conv_rows(j, outer, d1_ref, first, acc[0, j], acc[1, j])
            put_stats(i, q, s1, s2)
            return carry

        return body

    for p in range(k_in):
        with scope("P04halo1wait"):
            recv_rows(up1, down1, p)
        with scope("P05conv1outer"):
            lax.fori_loop(0, PER, conv1_outer(p), 0)
            start(at1 + p)
        if p > 0:
            with scope("P06relay1"):
                relay(at1 + p - 1)
    with scope("P06relay1"):
        relay(at1 + k_in - 1)

    def norm_to(src, act, i, k):
        def body(q, carry):
            lanes = lanes_of(k * PER + q)
            to = lanes_of(q)
            for b in range(pixels // step):
                span = slice(b * step, (b + 1) * step)
                act[k, span, to] = normal(src[span, lanes], i, q)
            return carry

        lax.fori_loop(0, PER, body, 0)

    def tile(act, w_ref, dst, k, n, fresh):
        deep = wide_of(k)
        wide = slice(n * CHUNK, (n + 1) * CHUNK)
        y = jnp.dot(act[k], w_ref[deep, wide], preferred_element_type=F32)
        if not fresh:
            y = y + dst[:, wide]
        dst[:, wide] = y
        return y

    def tile_stats(i, y):
        s1 = fold(y)
        s2 = fold(y * y)
        for q in range(PER):
            part = slice(q * LANES, (q + 1) * LANES)
            put_stats(i, q, s1[:, part], s2[:, part])

    load_w1_waited = False
    for k in range(k_in):
        with scope("P07finish1"):
            finish(at1 + k)
        with scope("P08norm1"):
            norm_to(first, act1, at1 + k, k)
        if k == 0:
            load_w1.wait()
        with scope("P09mm1"):
            for n in range(k_mid):
                y = tile(act1, w1_ref, second, k, n, k == 0)
                if k == k_in - 1:
                    tile_stats(at2 + n, y)
                    edge2[0, n] = y[pixels - edge :].astype(BF16)
                    edge2[1, n] = y[:edge].astype(BF16)
                    start(at2 + n)
                    if n >= LAG:
                        relay(at2 + n - LAG)
                        send_rows(up2, down2, n - LAG)
    with scope("P10relay2"):
        for n in range(max(k_mid - LAG, 0), k_mid):
            relay(at2 + n)
            send_rows(up2, down2, n)

    def conv2(n):
        def body(q, carry):
            i = at2 + n
            j = n * PER + q
            lanes = lanes_of(j)
            part = lanes_of(q)
            for r in range(rows):
                v = normal(second[r * cols : (r + 1) * cols, lanes], i, q)
                xp[j, r + RATE, PAD : PAD + cols, :] = v.astype(F32)
            top = normal(halo2[0, n, :, part].astype(F32), i, q).astype(F32)
            top = jnp.where(has_top, top, 0.0)
            bot = normal(halo2[1, n, :, part].astype(F32), i, q).astype(F32)
            bot = jnp.where(has_bot, bot, 0.0)
            for r in range(RATE):
                xp[j, r, PAD : PAD + cols, :] = top[r * cols : (r + 1) * cols]
                xp[j, rows + RATE + r, PAD : PAD + cols, :] = bot[r * cols : (r + 1) * cols]
            s1, s2 = conv_rows(j, list(range(rows)), d2_ref, second, zero8, zero8)
            put_stats(at3 + n, q, s1, s2)
            return carry

        return body

    for n in range(k_mid):
        with scope("P11finish2"):
            finish(at2 + n)
        with scope("P12edgewait"):
            recv_rows(up2, down2, n)
        with scope("P13conv2"):
            lax.fori_loop(0, PER, conv2(n), 0)
            start(at3 + n)
        if n > 0:
            with scope("P14relay3"):
                relay(at3 + n - 1)
    with scope("P14relay3"):
        relay(at3 + k_mid - 1)

    for k in range(k_mid):
        with scope("P15finish3"):
            finish(at3 + k)
        with scope("P16norm3"):
            norm_to(second, act3, at3 + k, k)
        if k == 0:
            load_w2.wait()
        with scope("P17mm2"):
            for n in range(k_out):
                y = tile(act3, w2_ref, fourth, k, n, k == 0)
                if k == k_mid - 1:
                    tile_stats(at4 + n, y)
                    start(at4 + n)
                    if n >= LAG:
                        relay(at4 + n - LAG)
    with scope("P18relay4"):
        for n in range(max(k_out - LAG, 0), k_out):
            relay(at4 + n)

    def last(n, carry):
        i = at4 + n
        finish(i)
        for q in range(PER):
            lanes = lanes_of(n * PER + q)
            for b in range(pixels // step):
                span = slice(b * step, (b + 1) * step)
                out[span, lanes] = normal(fourth[span, lanes], i, q)
        return carry

    with scope("P19last"):
        for n in range(k_out):
            last(n, 0)

    with scope("P20drain"):
        for p in range(k_in):
            sent_rows(up1, down1, p)
        for n in range(k_mid):
            sent_rows(up2, down2, n)
        for i in range(n_sum):
            near_sum(i).wait_send()
            far_all(i).wait_send()


def per_device(
    features,
    depth_one,
    gain_one,
    shift_one,
    point_one,
    gain_two,
    shift_two,
    depth_two,
    gain_three,
    shift_three,
    point_two,
    gain_four,
    shift_four,
):
    samples, span_rows, cols, c_in = features.shape
    rows = samples * span_rows
    assert samples == 1
    c_mid = point_one.shape[1]
    c_out = point_two.shape[1]
    pixels = rows * cols
    n_space = lax.axis_size("space")
    n_batch = lax.axis_size("batch")
    k_in, k_mid, k_out = c_in // CHUNK, c_mid // CHUNK, c_out // CHUNK
    n_sum = k_in + 2 * k_mid + k_out
    n_far = n_batch * n_space // 2
    any_spec = pl.BlockSpec(memory_space=pl.ANY)
    vmem = pl.BlockSpec(memory_space=pltpu.VMEM)
    edge = RATE * cols
    DMA = pltpu.SemaphoreType.DMA
    out = pl.pallas_call(
        functools.partial(kernel, n_space, n_batch),
        out_shape=pltpu.VMEM((pixels, c_out), BF16),
        in_specs=[any_spec] * 3 + [vmem] * 10,
        out_specs=vmem,
        scratch_shapes=[
            pltpu.VMEM((rows, cols, c_in), BF16),
            pltpu.VMEM((c_in, c_mid), BF16),
            pltpu.VMEM((c_mid, c_out), BF16),
            pltpu.VMEM((2, RATE, cols, c_in), BF16),
            pltpu.VMEM((2, k_mid, edge, CHUNK), BF16),
            pltpu.VMEM((2, k_mid, edge, CHUNK), BF16),
            pltpu.VMEM((c_mid // LANES, rows + 2 * RATE, cols + 2 * PAD, LANES), F32),
            pltpu.VMEM((pixels, c_in), F32),
            pltpu.VMEM((k_in, pixels, CHUNK), BF16),
            pltpu.VMEM((pixels, c_mid), F32),
            pltpu.VMEM((k_mid, pixels, CHUNK), BF16),
            pltpu.VMEM((pixels, c_out), F32),
            pltpu.VMEM((n_sum, 2 * PER, LANES), F32),
            pltpu.VMEM((n_sum, 2 * PER, LANES), F32),
            pltpu.VMEM((2, c_in // LANES, 8, LANES), F32),
            pltpu.VMEM((n_sum, 2, 2 * PER, LANES), F32),
            pltpu.VMEM((n_sum, n_far, 2 * PER, LANES), F32),
            DMA((2 + k_in,)),
            DMA((2,)),
            DMA((2, k_in)),
            DMA((2, k_in)),
            DMA((2, k_mid)),
            DMA((2, k_mid)),
            DMA((n_sum,)),
            DMA((n_sum,)),
            DMA((n_sum,)),
            DMA((n_sum,)),
        ],
        compiler_params=pltpu.CompilerParams(
            collective_id=0, has_side_effects=True, vmem_limit_bytes=56 * 1024 * 1024
        ),
        name="exit_block",
    )(
        features.reshape(rows, cols, c_in),
        point_one,
        point_two,
        depth_one,
        depth_two,
        gain_one,
        shift_one,
        gain_two,
        shift_two,
        gain_three,
        shift_three,
        gain_four,
        shift_four,
    )
    return out.reshape(samples, span_rows, cols, c_out)


def solution(mesh):
    return jax.shard_map(
        per_device,
        mesh=mesh,
        in_specs=(P("batch", "space", None, None),) + (P(),) * 12,
        out_specs=P("batch", "space", None, None),
        check_vma=False,
    )
```

time: 63.2 us -> 52.5 us (0.83)
  Pallas kernels: 59.3 us -> 50.5 us
  other arithmetic: 3.68 us -> 0 us
  local copies, waits for them, and re-layouts: 0 us -> 1.8 us
    pallas_call x1, Pallas kernels: 59.3 us -> 50.5 us  [per_device(): pl.pallas_call(functools.partial(kernel, n_space, n_batch), out_shape=plt...]
    convert_element_type x1 -> x0, other arithmetic: 3.68 us -> none  [per_device(): out = jnp.maximum((fourth - mean) * fac + shift, 0.0).astype(BF16)]
    unnamed x0 -> x1, local copies, waits for them, and re-layouts: none -> 1.8 us
where the time goes in v1:
time: 52.5 us; the launch traced here: 52.4 us
  Pallas kernels  50.5 us (96%)
  local copies, waits for them, and re-layouts  1.8 us (3%)
    pallas_call x1, Pallas kernels, per_device(): pl.pallas_call(functools.partial(kernel, n_space, n_batch), out_shape=plt...  50.5 us
    unnamed x1, local copies, waits for them, and re-layouts  1.8 us

profile of v1, /device:TPU:0, one launch (start us, length us, event | category | flops | bytes accessed | tf_op | source)
XLA Modules:
  0.0 52.4 jit_solution(9392515797317702907)
XLA Ops:
  0.0 50.5 %exit_block.1 = bf16[864,2048]{1,0:T(8,128)(2,1)S(1)} custom-call(bf16[12,72,1024]{2,1,0:T(8,128)(2,1)} %bitcast.3, bf16[1024,1536]{1,0:T(8,128)(2,1)} %w1_hbm.1, bf16[1536,2048]{1,0:T(8,128)(2,1)} %w2_hbm.1, bf16[3,3,1024]{2,1,0:T(4,128)(2,1)} %d1_ref.1, bf16[3,3,1536]{2,1,0:T(4,128)(2,1)} %d2_ref.1, f32[1024]{0:T(1024)} %g1_ref.1, f32[1024]{0:T(1024)} %b1_ref.1, ...), custom_call_target="tpu_custom_call" | custom-call | tf_op jit(solution)/shard_map/exit_block/pallas_call | solution.py:553
  50.6 1.8 %copy.15 = bf16[1,12,72,2048]{3,2,1,0:T(8,128)(2,1)} copy(bf16[1,12,72,2048]{3,2,1,0:T(8,128)(2,1)S(1)} %bitcast.2) | data formatting | bytes 7077888

commit v2 on v1

--- a/solution.py
+++ b/solution.py
@@ -13,7 +13,11 @@
 PAD = 8
 CHUNK = 256
 PER = CHUNK // LANES
-LAG = 4
+WIDE = 1
+TAIL = 2
+SLACK = 3
+DIRECT = 32
+ENDS = 2
 MESH = pl.DeviceIdType.MESH
 F32 = jnp.float32
 BF16 = jnp.bfloat16
@@ -25,6 +29,13 @@
         if pixels % rows == 0:
             return rows
     return pixels
+
+
+def lines_of(n_batch):
+    n_y = 1
+    while 8 * n_y * n_y <= n_batch and n_batch % (2 * n_y) == 0:
+        n_y *= 2
+    return n_y
 
 
 def kernel(
@@ -33,6 +44,17 @@
     x_hbm,
     w1_hbm,
     w2_hbm,
+    d1_hbm,
+    d2_hbm,
+    g1_hbm,
+    b1_hbm,
+    g2_hbm,
+    b2_hbm,
+    g3_hbm,
+    b3_hbm,
+    g4_hbm,
+    b4_hbm,
+    out,
     d1_ref,
     d2_ref,
     g1_ref,
@@ -43,7 +65,6 @@
     b3_ref,
     g4_ref,
     b4_ref,
-    out,
     x_ref,
     w1_ref,
     w2_ref,
@@ -63,6 +84,7 @@
     pb,
     x_sem,
     w_sem,
+    p_sem,
     h1_send,
     h1_recv,
     h2_send,
@@ -71,6 +93,8 @@
     a_recv,
     b_send,
     b_recv,
+    rise,
+    fall,
 ):
     rows, cols, c_in = x_hbm.shape
     c_mid = w1_hbm.shape[1]
@@ -91,27 +115,44 @@
     partner = sp + 1 - 2 * side
     has_top = sp > 0
     has_bot = sp < n_space - 1
-    odd = side == 1
-    cross = jnp.where(odd, sp + 1, sp - 1)
-    has_cross = jnp.logical_or(
-        jnp.logical_and(odd, has_bot), jnp.logical_and(jnp.logical_not(odd), has_top)
-    )
+    n_all = n_batch * n_space
+    self = bt * n_space + sp
+
+    def other(d):
+        at = lax.rem(self + d, n_all)
+        return {"batch": at // n_space, "space": lax.rem(at, n_space)}
 
     def far(d):
         at = lax.rem(mine + d, n_far)
         return {"batch": at // half, "space": lax.rem(at, half) * 2 + side}
 
-    def each_far(body):
-        if n_far <= 16:
-            for d in range(1, n_far):
+    n_y = lines_of(n_batch)
+    n_z = n_batch // n_y
+    n_plane = n_y * n_space
+    pos_z = bt // n_y
+    pos_plane = lax.rem(bt, n_y) * n_space + sp
+
+    def plane(d):
+        at = lax.rem(pos_plane + d, n_plane)
+        return {"batch": pos_z * n_y + at // n_space, "space": lax.rem(at, n_space)}
+
+    def line(d):
+        return {"batch": lax.rem(pos_z + d, n_z) * n_y + lax.rem(bt, n_y), "space": sp}
+
+    def each(count, body):
+        if count <= 32:
+            for d in range(1, count):
                 body(d)
         else:
 
-            def step_far(d, carry):
+            def step_one(d, carry):
                 body(d)
                 return carry
 
-            lax.fori_loop(1, n_far, step_far, 0)
+            lax.fori_loop(1, count, step_one, 0)
+
+    def each_other(body):
+        each(n_all, body)
 
     spans = [(0, RATE), (rows - RATE, RATE)]
     load_edges = [
@@ -128,21 +169,50 @@
     load_w1 = pltpu.make_async_copy(w1_hbm, w1_ref, w_sem.at[0])
     load_w2 = pltpu.make_async_copy(w2_hbm, w2_ref, w_sem.at[1])
 
+    small = (d1_hbm, d2_hbm, g1_hbm, b1_hbm, g2_hbm, b2_hbm, g3_hbm, b3_hbm, g4_hbm, b4_hbm)
+    small_to = (d1_ref, d2_ref, g1_ref, b1_ref, g2_ref, b2_ref, g3_ref, b3_ref, g4_ref, b4_ref)
+    load_small = [
+        pltpu.make_async_copy(a, b, p_sem.at[q]) for q, (a, b) in enumerate(zip(small, small_to))
+    ]
     for cp in load_edges:
         cp.start()
     for c in range(k_in):
         load_inner(c).start()
+    for cp in load_small:
+        cp.start()
+
+    below, above = pos_z > 0, pos_z < n_z - 1
+    inside = jnp.logical_and(below, above)
+
+    def tell(sem, device):
+        pl.semaphore_signal(sem, inc=1, device_id=device, device_id_type=MESH)
+
+    def tell_if(condition, sem, step_z):
+        @pl.when(condition)
+        def _():
+            tell(sem, {"batch": bt + step_z * n_y})
+
+    def wait_if(condition, sem):
+        @pl.when(condition)
+        def _():
+            pl.semaphore_wait(sem, 1)
 
     barrier = pltpu.get_barrier_semaphore()
-    pl.semaphore_signal(barrier, inc=1, device_id={"space": partner}, device_id_type=MESH)
-
-    @pl.when(has_cross)
-    def _():
-        pl.semaphore_signal(barrier, inc=1, device_id={"space": cross}, device_id_type=MESH)
-
-    each_far(
-        lambda d: pl.semaphore_signal(barrier, inc=1, device_id=far(d), device_id_type=MESH)
-    )
+    each(n_plane, lambda d: tell(barrier, plane(d)))
+    tell_if(below, barrier, -1)
+    tell_if(above, barrier, 1)
+    near = n_plane - 1 + jnp.where(below, 1, 0) + jnp.where(above, 1, 0)
+
+    rise_at = jnp.minimum(pos_z - 1, k_in - 2)
+    fall_at = jnp.where(pos_z == n_z - 2, 1, k_in - 1)
+
+    def meet(c):
+        now = rise_at == c
+        wait_if(jnp.logical_and(below, now), rise)
+        tell_if(jnp.logical_and(inside, now), rise, 1)
+        now = fall_at == c
+        wait_if(jnp.logical_and(above, now), fall)
+        tell_if(jnp.logical_and(inside, now), fall, -1)
 
     def clear(j, carry):
         for r in range(rows + 2 * RATE):
@@ -152,19 +222,13 @@
 
     with scope("P00clear"):
         lax.fori_loop(0, c_mid // LANES, clear, 0)
-        at = 0
-        for g_ref, b_ref in ((g1_ref, b1_ref), (g2_ref, b2_ref), (g3_ref, b3_ref), (g4_ref, b4_ref)):
-            for c in range(g_ref.shape[0] // CHUNK):
-                for q in range(PER):
-                    lanes = slice(c * CHUNK + q * LANES, c * CHUNK + (q + 1) * LANES)
-                    par[at, q : q + 1, :] = g_ref[lanes].reshape(1, LANES)
-                    par[at, PER + q : PER + q + 1, :] = b_ref[lanes].reshape(1, LANES)
-                at += 1
     with scope("P01edgewait"):
         for cp in load_edges:
             cp.wait()
     with scope("P02barrier"):
-        pl.semaphore_wait(barrier, n_far + jnp.where(has_cross, 1, 0))
+        pl.semaphore_wait(barrier, near)
+        tell_if(jnp.logical_and(above, jnp.logical_not(below)), rise, 1)
+        tell_if(jnp.logical_and(below, jnp.logical_not(above)), fall, -1)
 
     def up1(p):
         lanes = pl.ds(p * CHUNK, CHUNK)
@@ -248,48 +312,81 @@
         def _():
             halo[1] = jnp.zeros(halo.shape[1:], BF16)
 
-    def near_sum(i):
+    def kind(i):
+        if n_all > DIRECT:
+            return "grid"
+        if i in (at1, at2, at3, at3 + k_mid - 1):
+            return "one"
+        if at4 <= i < n_sum - ENDS or at2 + SLACK <= i < at3:
+            return "grid"
+        return "pair"
+
+    def home(i):
+        how = kind(i)
+        if how == "one":
+            return pb.at[i, self]
+        return pa.at[i, pos_plane] if how == "grid" else pa.at[i, side]
+
+    def hop(buf, i, slot, send, recv, device):
         return pltpu.make_async_remote_copy(
-            src_ref=pa.at[i, 0],
-            dst_ref=pa.at[i, 1],
-            send_sem=a_send.at[i],
-            recv_sem=a_recv.at[i],
-            device_id={"space": partner},
+            src_ref=buf.at[i, slot],
+            dst_ref=buf.at[i, slot],
+            send_sem=send.at[i],
+            recv_sem=recv.at[i],
+            device_id=device,
             device_id_type=MESH,
         )
 
-    def far_sum(i, d):
-        return pltpu.make_async_remote_copy(
-            src_ref=pb.at[i, mine],
-            dst_ref=pb.at[i, mine],
-            send_sem=b_send.at[i],
-            recv_sem=b_recv.at[i],
-            device_id=far(d),
-            device_id_type=MESH,
-        )
-
-    def far_all(i):
-        block = pb.at[i, pl.ds(0, n_far - 1)]
+    def bulk(buf, i, count, send, recv, device):
+        block = buf.at[i, pl.ds(0, count)]
         return pltpu.make_async_remote_copy(
             src_ref=block,
             dst_ref=block,
-            send_sem=b_send.at[i],
-            recv_sem=b_recv.at[i],
-            device_id=far(1),
+            send_sem=send.at[i],
+            recv_sem=recv.at[i],
+            device_id=device,
             device_id_type=MESH,
         )
 
+    def near_all(i):
+        if kind(i) == "grid":
+            return bulk(pa, i, n_plane - 1, a_send, a_recv, plane(1))
+        return bulk(pa, i, 1, a_send, a_recv, {"space": partner})
+
+    def far_count(i):
+        return {"one": n_all, "pair": n_far, "grid": n_z}[kind(i)]
+
+    def far_all(i):
+        device = {"one": other, "pair": far, "grid": line}[kind(i)](1)
+        return bulk(pb, i, far_count(i) - 1, b_send, b_recv, device)
+
     def start(i):
-        near_sum(i).start()
+        how = kind(i)
+        if how == "one":
+            each_other(lambda d: hop(pb, i, self, b_send, b_recv, other(d)).start())
+        elif how == "grid":
+            each(n_plane, lambda d: hop(pa, i, pos_plane, a_send, a_recv, plane(d)).start())
+        else:
+            hop(pa, i, side, a_send, a_recv, {"space": partner}).start()
 
     def relay(i):
-        near_sum(i).wait_recv()
-        pb[i, mine] = pa[i, 0] + pa[i, 1]
-        each_far(lambda d: far_sum(i, d).start())
+        how = kind(i)
+        if how == "one":
+            return
+        near_all(i).wait_recv()
+        if how == "grid":
+            s = pa[i, 0]
+            for k in range(1, n_plane):
+                s = s + pa[i, k]
+            pb[i, pos_z] = s
+            each(n_z, lambda d: hop(pb, i, pos_z, b_send, b_recv, line(d)).start())
+        else:
+            pb[i, mine] = pa[i, 0] + pa[i, 1]
+            each(n_far, lambda d: hop(pb, i, mine, b_send, b_recv, far(d)).start())
 
     def finish(i):
         far_all(i).wait_recv()
-        parts = [pb[i, k] for k in range(n_far)]
+        parts = [pb[i, k] for k in range(far_count(i))]
         while len(parts) > 1:
             parts = [a + b for a, b in zip(parts[0::2], parts[1::2])] + (
                 parts[-1:] if len(parts) % 2 else []
@@ -298,13 +395,12 @@
         mean = s[:PER]
         var = s[PER:] - mean * mean
         p = par[i]
-        coef[i, 0:PER] = mean
-        coef[i, PER : 2 * PER] = p[:PER] * lax.rsqrt(var + EPS)
+        fac = p[:PER] * lax.rsqrt(var + EPS)
+        coef[i, 0:PER] = fac
+        coef[i, PER : 2 * PER] = p[PER:] - mean * fac
 
     def normal(v, i, q):
-        mean = coef[i, pl.ds(q, 1), :]
-        fac = coef[i, pl.ds(PER + q, 1), :]
-        return jnp.maximum((v - mean) * fac + par[i, pl.ds(PER + q, 1), :], 0.0).astype(BF16)
+        return jnp.maximum(v * coef[i, pl.ds(q, 1), :] + coef[i, pl.ds(PER + q, 1), :], 0.0)
 
     def taps(d_ref, lanes):
         return [
@@ -320,9 +416,13 @@
         return y
 
     def lanes_of(j):
+        if isinstance(j, int):
+            return slice(j * LANES, (j + 1) * LANES)
         return pl.ds(pl.multiple_of(j * LANES, LANES), LANES)
 
     def wide_of(n):
+        if isinstance(n, int):
+            return slice(n * CHUNK, (n + 1) * CHUNK)
         return pl.ds(pl.multiple_of(n * CHUNK, CHUNK), CHUNK)
 
     def fold(v):
@@ -342,8 +442,9 @@
         return s1, s2
 
     def put_stats(i, q, s1, s2):
-        pa[i, 0, pl.ds(q, 1), :] = jnp.sum(s1, axis=0, keepdims=True)
-        pa[i, 0, pl.ds(PER + q, 1), :] = jnp.sum(s2, axis=0, keepdims=True)
+        to = home(i)
+        to[pl.ds(q, 1), :] = jnp.sum(s1, axis=0, keepdims=True)
+        to[pl.ds(PER + q, 1), :] = jnp.sum(s2, axis=0, keepdims=True)
 
     zero8 = jnp.zeros((8, LANES), F32)
     inner = list(range(RATE, rows - RATE))
@@ -358,12 +459,26 @@
         acc[1, j] = s2
         return carry
 
+    for cp in load_small[:2]:
+        cp.wait()
     for c in range(k_in):
         with scope("P03conv1inner"):
             load_inner(c).wait()
             lax.fori_loop(c * PER, (c + 1) * PER, conv1_inner, 0)
+        with scope("P03meet"):
+            meet(c)
     load_w1.start()
     load_w2.start()
+    for cp in load_small[2:]:
+        cp.wait()
+    at = 0
+    for g_ref, b_ref in ((g1_ref, b1_ref), (g2_ref, b2_ref), (g3_ref, b3_ref), (g4_ref, b4_ref)):
+        for c in range(g_ref.shape[0] // CHUNK):
+            for q in range(PER):
+                lanes = slice(c * CHUNK + q * LANES, c * CHUNK + (q + 1) * LANES)
+                par[at, q : q + 1, :] = g_ref[lanes].reshape(1, LANES)
+                par[at, PER + q : PER + q + 1, :] = b_ref[lanes].reshape(1, LANES)
+            at += 1
 
     def conv1_outer(i):
         def body(q, carry):
@@ -391,33 +506,38 @@
         relay(at1 + k_in - 1)
 
     def norm_to(src, act, i, k):
-        def body(q, carry):
-            lanes = lanes_of(k * PER + q)
-            to = lanes_of(q)
-            for b in range(pixels // step):
-                span = slice(b * step, (b + 1) * step)
-                act[k, span, to] = normal(src[span, lanes], i, q)
-            return carry
-
-        lax.fori_loop(0, PER, body, 0)
-
-    def tile(act, w_ref, dst, k, n, fresh):
-        deep = wide_of(k)
-        wide = slice(n * CHUNK, (n + 1) * CHUNK)
-        y = jnp.dot(act[k], w_ref[deep, wide], preferred_element_type=F32)
-        if not fresh:
-            y = y + dst[:, wide]
+        for b in range(pixels // step):
+            span = slice(b * step, (b + 1) * step)
+            for q in range(PER):
+                lanes = lanes_of(k * PER + q)
+                act[k, span, lanes_of(q)] = normal(src[span, lanes], i, q).astype(BF16)
+
+    def tile(act, w_ref, dst, ks, n0, n1, fresh):
+        wide = slice(n0 * CHUNK, n1 * CHUNK)
+        y = None if fresh else dst[:, wide]
+        for k in ks:
+            z = jnp.dot(act[k], w_ref[wide_of(k), wide], preferred_element_type=F32)
+            y = z if y is None else y + z
         dst[:, wide] = y
         return y
 
-    def tile_stats(i, y):
-        s1 = fold(y)
-        s2 = fold(y * y)
+    def pairs(count):
+        return [(n, min(n + WIDE, count)) for n in range(0, count, WIDE)]
+
+    def tile_sums(i, s1, s2):
         for q in range(PER):
             part = slice(q * LANES, (q + 1) * LANES)
             put_stats(i, q, s1[:, part], s2[:, part])
-
-    load_w1_waited = False
+        start(i)
+
+    def groups(count, first_ones):
+        at = 0
+        for size in first_ones:
+            if at + size < count:
+                yield list(range(at, at + size))
+                at += size
+        yield list(range(at, count))
+
     for k in range(k_in):
         with scope("P07finish1"):
             finish(at1 + k)
@@ -426,19 +546,24 @@
         if k == 0:
             load_w1.wait()
         with scope("P09mm1"):
-            for n in range(k_mid):
-                y = tile(act1, w1_ref, second, k, n, k == 0)
-                if k == k_in - 1:
-                    tile_stats(at2 + n, y)
+            if k < k_in - 1:
+                for n0, n1 in pairs(k_mid):
+                    tile(act1, w1_ref, second, (k,), n0, n1, k == 0)
+                continue
+            for group in groups(k_mid, (1, 2)):
+                sums = []
+                for n in group:
+                    y = tile(act1, w1_ref, second, (k,), n, n + 1, k == 0)
+                    sums.append((at2 + n, fold(y), fold(y * y)))
                     edge2[0, n] = y[pixels - edge :].astype(BF16)
                     edge2[1, n] = y[:edge].astype(BF16)
-                    start(at2 + n)
-                    if n >= LAG:
-                        relay(at2 + n - LAG)
-                        send_rows(up2, down2, n - LAG)
+                for s in sums:
+                    tile_sums(*s)
     with scope("P10relay2"):
-        for n in range(max(k_mid - LAG, 0), k_mid):
+        for n in range(min(SLACK, k_mid)):
             relay(at2 + n)
+            send_rows(up2, down2, n)
+        for n in range(SLACK, k_mid):
             send_rows(up2, down2, n)
 
     def conv2(n):
@@ -449,10 +574,10 @@
             part = lanes_of(q)
             for r in range(rows):
                 v = normal(second[r * cols : (r + 1) * cols, lanes], i, q)
-                xp[j, r + RATE, PAD : PAD + cols, :] = v.astype(F32)
-            top = normal(halo2[0, n, :, part].astype(F32), i, q).astype(F32)
+                xp[j, r + RATE, PAD : PAD + cols, :] = v
+            top = normal(halo2[0, n, :, part].astype(F32), i, q)
             top = jnp.where(has_top, top, 0.0)
-            bot = normal(halo2[1, n, :, part].astype(F32), i, q).astype(F32)
+            bot = normal(halo2[1, n, :, part].astype(F32), i, q)
             bot = jnp.where(has_bot, bot, 0.0)
             for r in range(RATE):
                 xp[j, r, PAD : PAD + cols, :] = top[r * cols : (r + 1) * cols]
@@ -471,9 +596,12 @@
         with scope("P13conv2"):
             lax.fori_loop(0, PER, conv2(n), 0)
             start(at3 + n)
-        if n > 0:
-            with scope("P14relay3"):
+        with scope("P14relay3"):
+            if n > 0:
                 relay(at3 + n - 1)
+            else:
+                for late in range(SLACK, k_mid):
+                    relay(at2 + late)
     with scope("P14relay3"):
         relay(at3 + k_mid - 1)
 
@@ -485,15 +613,20 @@
         if k == 0:
             load_w2.wait()
         with scope("P17mm2"):
-            for n in range(k_out):
-                y = tile(act3, w2_ref, fourth, k, n, k == 0)
-                if k == k_mid - 1:
-                    tile_stats(at4 + n, y)
-                    start(at4 + n)
-                    if n >= LAG:
-                        relay(at4 + n - LAG)
+            if k < k_mid - TAIL:
+                for n0, n1 in pairs(k_out):
+                    tile(act3, w2_ref, fourth, (k,), n0, n1, k == 0)
+            if k == k_mid - 1:
+                last_ks = tuple(range(max(k_mid - TAIL, 0), k_mid))
+                for group in groups(k_out, (3, 3)):
+                    sums = []
+                    for n in group:
+                        y = tile(act3, w2_ref, fourth, last_ks, n, n + 1, last_ks[0] == 0)
+                        sums.append((at4 + n, fold(y), fold(y * y)))
+                    for s in sums:
+                        tile_sums(*s)
     with scope("P18relay4"):
-        for n in range(max(k_out - LAG, 0), k_out):
+        for n in list(range(k_out - ENDS, k_out)) + list(range(k_out - ENDS)):
             relay(at4 + n)
 
     def last(n, carry):
@@ -503,11 +636,11 @@
             lanes = lanes_of(n * PER + q)
             for b in range(pixels // step):
                 span = slice(b * step, (b + 1) * step)
-                out[span, lanes] = normal(fourth[span, lanes], i, q)
+                out[span, lanes] = normal(fourth[span, lanes], i, q).astype(BF16)
         return carry
 
     with scope("P19last"):
-        for n in range(k_out):
+        for n in list(range(3)) + list(range(k_out - ENDS, k_out)) + list(range(3, k_out - ENDS)):
             last(n, 0)
 
     with scope("P20drain"):
@@ -516,7 +649,8 @@
         for n in range(k_mid):
             sent_rows(up2, down2, n)
         for i in range(n_sum):
-            near_sum(i).wait_send()
+            if kind(i) != "one":
+                near_all(i).wait_send()
             far_all(i).wait_send()
 
 
@@ -545,7 +679,8 @@
     n_batch = lax.axis_size("batch")
     k_in, k_mid, k_out = c_in // CHUNK, c_mid // CHUNK, c_out // CHUNK
     n_sum = k_in + 2 * k_mid + k_out
-    n_far = n_batch * n_space // 2
+    n_all = n_batch * n_space
+    slots = n_all if n_all <= DIRECT else n_batch // lines_of(n_batch)
     any_spec = pl.BlockSpec(memory_space=pl.ANY)
     vmem = pl.BlockSpec(memory_space=pltpu.VMEM)
     edge = RATE * cols
@@ -553,9 +688,14 @@
     out = pl.pallas_call(
         functools.partial(kernel, n_space, n_batch),
         out_shape=pltpu.VMEM((pixels, c_out), BF16),
-        in_specs=[any_spec] * 3 + [vmem] * 10,
+        in_specs=[any_spec] * 13,
         out_specs=vmem,
         scratch_shapes=[
+            pltpu.VMEM(depth_one.shape, BF16),
+            pltpu.VMEM(depth_two.shape, BF16),
+        ]
+        + [pltpu.VMEM((c,), F32) for c in (c_in, c_in, c_mid, c_mid, c_mid, c_mid, c_out, c_out)]
+        + [
             pltpu.VMEM((rows, cols, c_in), BF16),
             pltpu.VMEM((c_in, c_mid), BF16),
             pltpu.VMEM((c_mid, c_out), BF16),
@@ -571,10 +711,11 @@
             pltpu.VMEM((n_sum, 2 * PER, LANES), F32),
             pltpu.VMEM((n_sum, 2 * PER, LANES), F32),
             pltpu.VMEM((2, c_in // LANES, 8, LANES), F32),
-            pltpu.VMEM((n_sum, 2, 2 * PER, LANES), F32),
-            pltpu.VMEM((n_sum, n_far, 2 * PER, LANES), F32),
+            pltpu.VMEM((n_sum, lines_of(n_batch) * n_space, 2 * PER, LANES), F32),
+            pltpu.VMEM((n_sum, slots, 2 * PER, LANES), F32),
             DMA((2 + k_in,)),
             DMA((2,)),
+            DMA((10,)),
             DMA((2, k_in)),
             DMA((2, k_in)),
             DMA((2, k_mid)),
@@ -583,6 +724,8 @@
             DMA((n_sum,)),
             DMA((n_sum,)),
             DMA((n_sum,)),
+            pltpu.SemaphoreType.REGULAR,
+            pltpu.SemaphoreType.REGULAR,
         ],
         compiler_params=pltpu.CompilerParams(
             collective_id=0, has_side_effects=True, vmem_limit_bytes=56 * 1024 * 1024

time: 52.5 us -> 47.8 us (0.910)
  Pallas kernels: 50.5 us -> 45.9 us
    pallas_call x1, Pallas kernels: 50.5 us -> 45.9 us  [per_device(): pl.pallas_call(functools.partial(kernel, n_space, n_batch), out_shape=plt...]
where the time goes in v2:
time: 47.8 us; the launch traced here: 47.7 us
  Pallas kernels  45.9 us (96%)
  local copies, waits for them, and re-layouts  1.8 us (4%)
    pallas_call x1, Pallas kernels, per_device(): pl.pallas_call(functools.partial(kernel, n_space, n_batch), out_shape=plt...  45.9 us
    unnamed x1, local copies, waits for them, and re-layouts  1.8 us

profile of v2, /device:TPU:0, one launch (start us, length us, event | category | flops | bytes accessed | tf_op | source)
XLA Modules:
  0.0 47.7 jit_solution(1367733587121187536)
XLA Ops:
  0.0 45.9 %exit_block.1 = bf16[864,2048]{1,0:T(8,128)(2,1)S(1)} custom-call(bf16[12,72,1024]{2,1,0:T(8,128)(2,1)} %bitcast.3, bf16[1024,1536]{1,0:T(8,128)(2,1)} %w1_hbm.1, bf16[1536,2048]{1,0:T(8,128)(2,1)} %w2_hbm.1, bf16[3,3,1024]{2,1,0:T(4,128)(2,1)} %d1_hbm.1, bf16[3,3,1536]{2,1,0:T(4,128)(2,1)} %d2_hbm.1, f32[1024]{0:T(1024)} %g1_hbm.1, f32[1024]{0:T(1024)} %b1_hbm.1, ...), custom_call_target="tpu_custom_call" | custom-call | tf_op jit(solution)/shard_map/exit_block/pallas_call | solution.py:688
  45.9 1.8 %copy.15 = bf16[1,12,72,2048]{3,2,1,0:T(8,128)(2,1)} copy(bf16[1,12,72,2048]{3,2,1,0:T(8,128)(2,1)S(1)} %bitcast.2) | data formatting | bytes 7077888

commit v3 on v2

--- a/solution.py
+++ b/solution.py
@@ -17,7 +17,7 @@
 TAIL = 2
 SLACK = 3
 DIRECT = 32
-ENDS = 2
+ENDS = 4
 MESH = pl.DeviceIdType.MESH
 F32 = jnp.float32
 BF16 = jnp.bfloat16
@@ -560,10 +560,8 @@
                 for s in sums:
                     tile_sums(*s)
     with scope("P10relay2"):
-        for n in range(min(SLACK, k_mid)):
+        for n in range(k_mid):
             relay(at2 + n)
-            send_rows(up2, down2, n)
-        for n in range(SLACK, k_mid):
             send_rows(up2, down2, n)
 
     def conv2(n):
@@ -599,9 +597,6 @@
         with scope("P14relay3"):
             if n > 0:
                 relay(at3 + n - 1)
-            else:
-                for late in range(SLACK, k_mid):
-                    relay(at2 + late)
     with scope("P14relay3"):
         relay(at3 + k_mid - 1)
 
@@ -618,7 +613,7 @@
                     tile(act3, w2_ref, fourth, (k,), n0, n1, k == 0)
             if k == k_mid - 1:
                 last_ks = tuple(range(max(k_mid - TAIL, 0), k_mid))
-                for group in groups(k_out, (3, 3)):
+                for group in groups(k_out, (4,)):
                     sums = []
                     for n in group:
                         y = tile(act3, w2_ref, fourth, last_ks, n, n + 1, last_ks[0] == 0)

time: 47.8 us -> 46.3 us (0.969)
  Pallas kernels: 45.9 us -> 44.4 us
    pallas_call x1, Pallas kernels: 45.9 us -> 44.4 us  [per_device(): pl.pallas_call(functools.partial(kernel, n_space, n_batch), out_shape=plt...]
where the time goes in v3:
time: 46.3 us; the launch traced here: 46.2 us
  Pallas kernels  44.4 us (96%)
  local copies, waits for them, and re-layouts  1.8 us (4%)
    pallas_call x1, Pallas kernels, per_device(): pl.pallas_call(functools.partial(kernel, n_space, n_batch), out_shape=plt...  44.4 us
    unnamed x1, local copies, waits for them, and re-layouts  1.8 us

profile of v3, /device:TPU:0, one launch (start us, length us, event | category | flops | bytes accessed | tf_op | source)
XLA Modules:
  0.0 46.2 jit_solution(11143897424005743167)
XLA Ops:
  0.0 44.4 %exit_block.1 = bf16[864,2048]{1,0:T(8,128)(2,1)S(1)} custom-call(bf16[12,72,1024]{2,1,0:T(8,128)(2,1)} %bitcast.3, bf16[1024,1536]{1,0:T(8,128)(2,1)} %w1_hbm.1, bf16[1536,2048]{1,0:T(8,128)(2,1)} %w2_hbm.1, bf16[3,3,1024]{2,1,0:T(4,128)(2,1)} %d1_hbm.1, bf16[3,3,1536]{2,1,0:T(4,128)(2,1)} %d2_hbm.1, f32[1024]{0:T(1024)} %g1_hbm.1, f32[1024]{0:T(1024)} %b1_hbm.1, ...), custom_call_target="tpu_custom_call" | custom-call | tf_op jit(solution)/shard_map/exit_block/pallas_call | solution.py:683
  44.4 1.8 %copy.15 = bf16[1,12,72,2048]{3,2,1,0:T(8,128)(2,1)} copy(bf16[1,12,72,2048]{3,2,1,0:T(8,128)(2,1)S(1)} %bitcast.2) | data formatting | bytes 7077888
